TPU v7x, 32 devices: a whole 2x2x4 slice. The times are simulated.
32 devices in a mesh: wide: 8 (over y, x, core), narrow: 4 (over z).
Axes of the slice: x: 2, y: 2, z: 4, core: 2. Of those that a mesh axis runs over, the one named last changes fastest.
Arguments:
- hamiltonian: float32 [64, 3, 128, 128], P(('wide', 'narrow')), may hold values from -3.3 to 3.3, as said below
- old_density: float32 [64, 3, 128, 128], P(('wide', 'narrow')), may hold values from -2 to 2
- neighbours: int32 [64, 3], P(('wide', 'narrow')), may hold values from 0 to 7, as said below
- live: int32 [64], P(('wide', 'narrow')), may hold values from 0 to 1, as said below
- potential: float32 [1], replicated, may hold values from -1 to 1
Outputs:
- density: float32 [64, 3, 128, 128], P(('wide', 'narrow'))
Inputs may be any that keep to these rules, and one draw needn't show every extreme that they name: Within each cluster of 8 consecutive blocks, entry 0 is the block's own index in the cluster and entries 1 and 2 are its neighbours on a cycle through all blocks of the cluster: block a is entry 1 of its entry-2 neighbour and entry 2 of its entry-1 neighbour. Along the cycle the 2 blocks of one device stand next to each other in some order; the devices of the narrow axis follow each other in an order drawn from the seed. For each index of the narrow axis, the devices at wide indices i and i + 4 own at most 2 live blocks together; in every draw some device owns 2 live blocks. `hamiltonian`: the block Hamiltonian is symmetric: tile 1 of block c is the transpose of tile 2 of prev(c), and tile 0 is symmetric.
All inputs are finite; a program needn't handle non-finite values. Where the computation divides by a largest or mean magnitude, that divisor is 1e-20 or more.
Results may differ from a plain program's by a relative error of at most 0.0001.
Values sent between devices are 32-bit elements; how exact they have to be, the bound alone decides.
No kernel may reach another device: no remote copies, remote signals or barrier semaphores. Data moves between devices by JAX's collectives and lax.ppermute only.
A program may use at most 64 MiB of HBM per device.

v0:
```python
import jax
import jax.numpy as jnp
from jax import lax
from jax.sharding import PartitionSpec as P

ITERS = 4


epsilon = 1e-06


def product(left, right):
    return jnp.matmul(left, right, precision=lax.Precision.HIGHEST)


def transpose_tiles(tiles):
    return jnp.swapaxes(tiles, -1, -2)


def assemble(row_tiles, prev_onsite, next_onsite, level):
    zero_tile = jnp.zeros_like(prev_onsite)
    upper_rows = jnp.concatenate(
        [row_tiles[..., 0, :, :], row_tiles[..., 1, :, :], row_tiles[..., 2, :, :]], axis=-1
    )
    middle_rows = jnp.concatenate(
        [transpose_tiles(row_tiles[..., 1, :, :]), prev_onsite, zero_tile], axis=-1
    )
    lower_rows = jnp.concatenate(
        [transpose_tiles(row_tiles[..., 2, :, :]), zero_tile, next_onsite], axis=-1
    )
    matrix = jnp.concatenate([upper_rows, middle_rows, lower_rows], axis=-2)
    order = matrix.shape[-1]
    return matrix - level * jnp.eye(order, dtype=jnp.float32)


def sign_columns(matrix, width, depth):
    order = matrix.shape[-1]
    identity = jnp.eye(order, dtype=jnp.float32)
    bound = jnp.max(jnp.sum(jnp.abs(matrix), axis=-1), axis=-1) + epsilon
    current = matrix / bound[..., None, None]
    for sweep in range(depth - 1):
        square = product(current, current)
        current = 0.5 * product(current, 3.0 * identity - square)
    square = product(current, current)
    final_cols = 0.5 * product(current, 3.0 * identity[:, :width] - square[..., :, :width])
    columns = 0.5 * (identity[:, :width] - final_cols)
    return columns.reshape(columns.shape[:-2] + (order // width, width, width))


def shards(hamiltonian, old_density, neighbours, live, potential):
    width = hamiltonian.shape[-1]
    level = potential[0]
    cluster_onsite = lax.all_gather(hamiltonian[:, 0], "narrow", axis=0, tiled=True)
    prev_onsite = jnp.take(cluster_onsite, neighbours[:, 1], axis=0)
    next_onsite = jnp.take(cluster_onsite, neighbours[:, 2], axis=0)
    matrices = assemble(hamiltonian, prev_onsite, next_onsite, level)
    new_cols = sign_columns(matrices, width, ITERS)
    fresh_cols = jnp.where(live[:, None, None, None] == 1, new_cols, old_density)
    prev_side, next_side = (
        lax.all_gather(fresh_cols[:, 1], "narrow", axis=0, tiled=True),
        lax.all_gather(fresh_cols[:, 2], "narrow", axis=0, tiled=True),
    )
    from_prev = jnp.take(next_side, neighbours[:, 1], axis=0)
    from_next = jnp.take(prev_side, neighbours[:, 2], axis=0)
    return jnp.stack(
        [
            0.5 * (fresh_cols[:, 0] + transpose_tiles(fresh_cols[:, 0])),
            0.5 * (fresh_cols[:, 1] + transpose_tiles(from_prev)),
            0.5 * (fresh_cols[:, 2] + transpose_tiles(from_next)),
        ],
        axis=1,
    )


def solution(mesh):
    placed = (
        P(("wide", "narrow"), None, None, None),
        P(("wide", "narrow"), None, None, None),
        P(("wide", "narrow"), None),
        P(("wide", "narrow")),
        P(),
    )
    return jax.shard_map(
        shards,
        mesh=mesh,
        in_specs=placed,
        out_specs=P(("wide", "narrow"), None, None, None),
        check_vma=False,
    )
```

profile of v0, /device:TPU:0, one launch (start us, length us, event | category | flops | bytes accessed | tf_op | source)
XLA Modules:
  0.0 73.8 jit_solution(11222898801294585390)
XLA Ops:
  0.0 1.1 %slice_bitcast_fusion.6 = (f32[2,128,128]{2,1,0:T(8,128)S(1)}, f32[2,128,128]{2,1,0:T(8,128)S(1)}, f32[2,128,128]{2,1,0:T(8,128)S(1)}, f32[2,1,128,128]{3,2,1,0:...) fusion(f32[2,3,128,128]{3,2,1,0:T(8,128)} %param.7), kind=kLoop, calls=%fused_computation.51 | loop fusion | bytes 1179648 | tf_op jit(solution)/shard_map/squeeze | solution.py:23
  1.1 17.4 %all-gather = f32[8,1,128,128]{3,2,1,0:T(8,128)S(1)} all-gather(f32[2,1,128,128]{3,2,1,0:T(8,128)S(1)} %get-tuple-element.15), channel_id=2, replica_groups=mesh['wide'=8,'narrow'=4] {'narrow'}, dimensions={0}, use_global_device_ids=true | all-gather | bytes 655360 | tf_op jit(solution)/shard_map/all_gather | solution.py:53
  18.5 0.2 slice_reduce_fusion.1
  18.7 0.6 gather_fusion.1
  19.3 0.1 broadcast_select_fusion
  19.4 0.6 gather_fusion
  20.0 0.1 broadcast_select_fusion.1
  20.1 0.1 copy.88
  20.2 0.1 copy.89
  21.0 0.2 abs_reduce_fusion
  21.2 0.1 reduce_max.9
  21.4 2.6 %convolution_subtract_fusion.2 = f32[2,384,384]{2,1,0:T(8,128)S(1)} fusion(f32[384,384]{1,0:T(8,128)S(1)} %fusion.3, f32[2]{0:T(128)S(1)} %broadcast_add_fusion, f32[2,128,128]{2,1,0:T(8,128)S(1)} %broadcast_select_fusion, f32[2,128,128]{2,1,0:T(8,128)S(1)} %broadcast_in_dim.17, f32[2,128,128]{2,1,0:T(8,128)S(1)} %bitcast.74, ...), kind=kOutput, calls=%fused_computation.9 | convolution fusion | flops 1362198528 | bytes 3407880 | tf_op jit(solution)/shard_map/dot_general | solution.py:13
  24.0 2.5 %convolution_multiply_fusion.2 = f32[2,384,384]{2,1,0:T(8,128)S(1)} fusion(f32[2,384,384]{2,1,0:T(8,128)S(1)} %convolution_subtract_fusion.2, f32[2]{0:T(128)S(1)} %broadcast_add_fusion, f32[2,128,128]{2,1,0:T(8,128)S(1)} %broadcast_select_fusion, f32[2,128,128]{2,1,0:T(8,128)S(1)} %broadcast_in_dim.17, f32[2,128,128]{2,1,0:T(8,128)S(1)} %bitcast.75, ...), kind=kOutput, calls=%fused_computation.8 | convolution fusion | flops 1362198528 | bytes 3997704 | tf_op jit(solution)/shard_map/dot_general | solution.py:13
  26.5 2.5 %convolution_subtract_fusion.1 = f32[2,384,384]{2,1,0:T(8,128)S(1)} fusion(f32[2,384,384]{2,1,0:T(8,128)S(1)} %convolution_multiply_fusion.2, f32[384,384]{1,0:T(8,128)S(1)} %fusion.3), kind=kOutput, calls=%fused_computation.7 | convolution fusion | flops 1359249408 | bytes 2949120 | tf_op jit(solution)/shard_map/dot_general | solution.py:13
  29.0 2.4 %convolution_multiply_fusion.1 = f32[2,384,384]{2,1,0:T(8,128)S(1)} fusion(f32[2,384,384]{2,1,0:T(8,128)S(1)} %convolution_multiply_fusion.2, f32[2,384,384]{2,1,0:T(8,128)S(1)} %convolution_subtract_fusion.1), kind=kOutput, calls=%fused_computation.6 | convolution fusion | flops 1359249408 | bytes 3538944 | tf_op jit(solution)/shard_map/dot_general | solution.py:13
  31.4 2.7 %convolution_subtract_fusion = f32[2,384,384]{2,1,0:T(8,128)S(1)} fusion(f32[2,384,384]{2,1,0:T(8,128)S(1)} %convolution_multiply_fusion.1, f32[384,384]{1,0:T(8,128)S(1)} %fusion.3), kind=kOutput, calls=%fused_computation.5 | convolution fusion | flops 1359249408 | bytes 2949120 | tf_op jit(solution)/shard_map/dot_general | solution.py:13
  34.1 2.4 %convolution_multiply_fusion = f32[2,384,384]{2,1,0:T(8,128)S(1)} fusion(f32[2,384,384]{2,1,0:T(8,128)S(1)} %convolution_multiply_fusion.1, f32[2,384,384]{2,1,0:T(8,128)S(1)} %convolution_subtract_fusion), kind=kOutput, calls=%fused_computation.4 | convolution fusion | flops 1359249408 | bytes 3538944 | tf_op jit(solution)/shard_map/dot_general | solution.py:13
  36.6 1.2 %convolution_subtract_fusion.3 = f32[2,384,128]{2,1,0:T(8,128)S(1)} fusion(f32[2,384,384]{2,1,0:T(8,128)S(1)} %convolution_multiply_fusion, f32[384,128]{1,0:T(8,128)S(1)} %slice_select_fusion), kind=kOutput, calls=%fused_computation.10 | convolution fusion | flops 453083136 | bytes 2162688 | tf_op jit(solution)/shard_map/dot_general | solution.py:13
  37.8 0.0 copy-start.2
  37.9 1.2 %fusion.1 = f32[2,384,128]{2,1,0:T(8,128)S(1)} fusion(f32[2,384,384]{2,1,0:T(8,128)S(1)} %convolution_multiply_fusion, f32[2,384,128]{2,1,0:T(8,128)S(1)} %convolution_subtract_fusion.3, f32[384,128]{1,0:T(8,128)S(1)} %slice_convert_fusion), kind=kOutput, calls=%fused_computation.13 | convolution fusion | flops 453279744 | bytes 2162688 | tf_op jit(solution)/shard_map/dot_general | solution.py:13
  39.1 0.1 copy_select_fusion
  39.3 0.1 copy.80
  39.4 16.2 %all-gather.1 = f32[8,1,128,128]{3,2,1,0:T(8,128)S(1)} all-gather(f32[2,1,128,128]{3,2,1,0:T(8,128)S(1)} %get-tuple-element.10), channel_id=3, replica_groups=mesh['wide'=8,'narrow'=4] {'narrow'}, dimensions={0}, use_global_device_ids=true | all-gather | bytes 655360 | tf_op jit(solution)/shard_map/all_gather | solution.py:61
  55.6 0.6 gather_fusion.2
  56.2 0.1 copy.82
  56.3 0.1 fusion.8
  56.4 15.6 %all-gather.2 = f32[8,1,128,128]{3,2,1,0:T(8,128)S(1)} all-gather(f32[2,1,128,128]{3,2,1,0:T(8,128)S(1)} %get-tuple-element.9), channel_id=4, replica_groups=mesh['wide'=8,'narrow'=4] {'narrow'}, dimensions={0}, use_global_device_ids=true | all-gather | bytes 655360 | tf_op jit(solution)/shard_map/all_gather | solution.py:60
  72.0 0.6 gather_fusion.3
  72.5 0.1 copy.84
  72.6 0.1 bitcast_add_fusion.1
  72.7 0.1 copy.85
  72.9 0.9 %copy.86 = f32[2,3,128,128]{3,2,1,0:T(8,128)} copy(f32[2,3,128,128]{2,3,0,1:T(8,128)S(1)} %pad_maximum_fusion) | data formatting | bytes 786432 | tf_op jit(solution)/shard_map/stack | solution.py:65
  (21 shorter events, 0.3 us)
Async XLA Ops:
  0.0 18.5 %copy-start.1 = (s32[2,3]{1,0:T(2,128)S(1)}, s32[2,3]{1,0:T(2,128)}, u32[]{:S(2)}) copy-start(s32[2,3]{1,0:T(2,128)} %param.9) | copy-start | bytes 76
  37.8 1.2 %copy-start.2 = (s32[2]{0:T(128)S(1)}, s32[2]{0:T(128)}, u32[]{:S(2)}) copy-start(s32[2]{0:T(128)} %param.10) | copy-start | bytes 28
  37.8 1.3 %copy-start = (f32[2,3,128,128]{3,2,1,0:T(8,128)S(1)}, f32[2,3,128,128]{3,2,1,0:T(8,128)}, u32[]{:S(2)}) copy-start(f32[2,3,128,128]{3,2,1,0:T(8,128)} %param.8) | copy-start | bytes 1179652
where the time goes:
time: 74 us; the launch traced here: 73.8 us
  blocking collectives  49.2 us (66%)
  matrix products  17.5 us (24%)
  local copies, waits for them, and re-layouts  5.08 us (7%)
  other arithmetic  1.06 us (1%)
  between operations  0.96 us (1%)
    dot_general x8, matrix products, product(): return jnp.matmul(left, right, precision=lax.Precision.HIGHEST)  17.5 us
    all_gather x1, blocking collectives, shards(): lax.all_gather(hamiltonian[:, 0], 'narrow', axis=0, tiled=True)  17.4 us
    all_gather x1, blocking collectives, shards(): lax.all_gather(fresh_cols[:, 2], 'narrow', axis=0, tiled=True)  16.2 us
    all_gather x1, blocking collectives, shards(): lax.all_gather(fresh_cols[:, 1], 'narrow', axis=0, tiled=True)  15.6 us

commit v1 on v0

v1 whole, which is shorter than its diff:
```python
import functools

import jax
import jax.numpy as jnp
from jax import lax
from jax.experimental import pallas as pl
from jax.experimental.pallas import tpu as pltpu
from jax.sharding import PartitionSpec as P

ITERS = 4
EPSILON = 1e-06
VMEM = pltpu.VMEM
SMEM = pltpu.SMEM


def peer(me, k, n):
    if n & (n - 1) == 0:
        return me ^ k, me ^ k
    return lax.rem(me + k, n), lax.rem(me + n - k, n)


def pairs(k, n):
    if n & (n - 1) == 0:
        return [(i, i ^ k) for i in range(n)]
    return [(i, (i + k) % n) for i in range(n)]


def roles(nb_ref, per):
    me = lax.axis_index("narrow")
    first = jnp.where(lax.div(nb_ref[0, 1], per) == me, 1, 0)
    last = 1 - first
    dev_prev = lax.div(nb_ref[first, 1], per)
    dev_next = lax.div(nb_ref[last, 2], per)
    return me, first, last, dev_prev, dev_next


def iota(shape, dim):
    return lax.broadcasted_iota(jnp.int32, shape, dim)


def pack(tile):
    w = tile.shape[0]
    h = w // 2
    top, low = tile[:h], tile[h:]
    low_left = jnp.concatenate([low[:, h:], low[:, :h]], axis=1)
    rows, cols = iota((h, w), 0), iota((h, w), 1)
    body = jnp.where(cols < rows, low_left, top)
    diag = jnp.sum(jnp.where(cols == rows, low_left, 0.0), axis=0, keepdims=True)
    return body, jnp.broadcast_to(diag, (8, w))


def unpack(body, diag):
    h, w = body.shape
    rows, cols = iota((h, w), 0), iota((h, w), 1)
    flipped = body.T
    mirror = jnp.concatenate([flipped[:h], flipped[:h]], axis=1)
    top = jnp.where(cols < rows, mirror, body)
    swapped = jnp.concatenate([body[:, h:], body[:, :h]], axis=1)
    col_low = cols - h
    right = jnp.where(col_low < rows, swapped, mirror)
    diag_right = jnp.concatenate([diag[:1, h:], diag[:1, :h]], axis=1)
    right = jnp.where(col_low == rows, jnp.broadcast_to(diag_right, (h, w)), right)
    low = jnp.where(cols < h, jnp.concatenate([flipped[h:], flipped[h:]], axis=1), right)
    return jnp.concatenate([top, low], axis=0)


def pack_kernel(n, nb_ref, h_ref, *out_refs):
    per, _, w, _ = h_ref.shape
    me, first, last, dev_prev, _ = roles(nb_ref, per)
    h = w // 2
    bodies, diags = zip(*[pack(h_ref[b, 0]) for b in range(per)])
    for k in range(1, n):
        to, _ = peer(me, k, n)
        chosen = jnp.where(dev_prev == to, first, last)
        out_refs[k - 1][:h] = jnp.where(chosen == 0, bodies[0], bodies[1])
        out_refs[k - 1][h:] = jnp.where(chosen == 0, diags[0], diags[1])


def split(x):
    high = x.astype(jnp.bfloat16)
    low = (x - high.astype(jnp.float32)).astype(jnp.bfloat16)
    return high, low


def dot(a, b):
    return jnp.dot(a, b, preferred_element_type=jnp.float32)


def product(a, b):
    ah, al = a
    bh, bl = b
    return dot(
        jnp.concatenate([ah, ah, al], axis=1), jnp.concatenate([bh, bl, bh], axis=0)
    )


def start_matrix(onsite, near, far, near_onsite, far_onsite, level):
    w = onsite.shape[0]
    zero = jnp.zeros((w, w), jnp.float32)
    matrix = jnp.concatenate(
        [
            jnp.concatenate([onsite, near, far], axis=1),
            jnp.concatenate([near.T, near_onsite, zero], axis=1),
            jnp.concatenate([far.T, zero, far_onsite], axis=1),
        ],
        axis=0,
    )
    order = matrix.shape[0]
    eye = jnp.where(iota((order, order), 0) == iota((order, order), 1), 1.0, 0.0)
    matrix = matrix - level * eye
    rows = jnp.sum(jnp.abs(matrix), axis=1, keepdims=True)
    bound = jnp.max(rows, axis=0, keepdims=True) + EPSILON
    return matrix * (1.0 / bound), eye


def main_kernel(n, nb_ref, live_ref, pot_ref, h_ref, old_ref, *refs):
    got, (dens_ref, half_ref), out_refs = refs[: n - 1], refs[n - 1 : n + 1], refs[n + 1 :]
    per, _, w, _ = h_ref.shape
    h = w // 2
    me, first, last, dev_prev, dev_next = roles(nb_ref, per)
    level = pot_ref[0]

    def received(source):
        body, diag = got[0][:h], got[0][h:]
        for k in range(2, n):
            _, origin = peer(me, k, n)
            body = jnp.where(origin == source, got[k - 1][:h], body)
            diag = jnp.where(origin == source, got[k - 1][h:], diag)
        return unpack(body, diag)

    from_prev, from_next = received(dev_prev), received(dev_next)
    blocks = []
    for own, other, near, far, remote in (
        (first, last, 2, 1, from_prev),
        (last, first, 1, 2, from_next),
    ):
        x, eye = start_matrix(
            h_ref[own, 0], h_ref[own, near], h_ref[own, far], h_ref[other, 0], remote, level
        )
        blocks.append(x)
    for sweep in range(ITERS - 1):
        for i in range(2):
            x = split(blocks[i])
            square = product(x, x)
            blocks[i] = product(x, split(1.5 * eye - 0.5 * square))
    fresh = []
    for i, (own, near, far) in enumerate(((first, 2, 1), (last, 1, 2))):
        xh, xl = split(blocks[i])
        square = product((xh, xl), (xh[:, :w], xl[:, :w]))
        cols = product((xh, xl), split(1.5 * eye[:, :w] - 0.5 * square))
        cols = 0.5 * (eye[:, :w] - cols)
        alive = live_ref[own] == 1
        fresh.append(
            [
                jnp.where(alive, cols[r * w : (r + 1) * w], old_ref[own, slot])
                for r, slot in enumerate((0, near, far))
            ]
        )
    (f0, f_near, f_far), (l0, l_near, l_far) = fresh
    half_ref[0] = 0.5 * f_far
    half_ref[1] = 0.5 * l_far
    f_send, l_send = (0.5 * f_far).T, (0.5 * l_far).T
    for k in range(1, n):
        to, _ = peer(me, k, n)
        out_refs[k - 1][...] = jnp.where(dev_prev == to, f_send, l_send)
    dens_ref[first, 0] = 0.5 * (f0 + f0.T)
    dens_ref[last, 0] = 0.5 * (l0 + l0.T)
    edge = 0.5 * (f_near + l_near.T)
    dens_ref[first, 2] = edge
    dens_ref[last, 1] = edge.T
    dens_ref[first, 1] = jnp.zeros_like(edge)
    dens_ref[last, 2] = jnp.zeros_like(edge)


def final_kernel(n, nb_ref, half_ref, dens_in, *refs):
    got, dens_ref, buf, sems = refs[: n - 1], refs[n - 1], refs[n], refs[n + 1]
    me, first, last, dev_prev, dev_next = roles(nb_ref, 2)

    def received(source):
        tile = got[0][...]
        for k in range(2, n):
            _, origin = peer(me, k, n)
            tile = jnp.where(origin == source, got[k - 1][...], tile)
        return tile

    buf[0] = half_ref[0] + received(dev_prev)
    one = pltpu.make_async_copy(buf.at[0], dens_ref.at[first, 1], sems.at[0])
    one.start()
    buf[1] = half_ref[1] + received(dev_next)
    two = pltpu.make_async_copy(buf.at[1], dens_ref.at[last, 2], sems.at[1])
    two.start()
    one.wait()
    two.wait()


def vspec():
    return pl.BlockSpec(memory_space=VMEM)


def sspec():
    return pl.BlockSpec(memory_space=SMEM)


def shards(n, hamiltonian, old_density, neighbours, live, potential):
    per, _, w, _ = hamiltonian.shape
    assert per == 2 and n > 2
    f32 = jnp.float32
    diag_msgs = pl.pallas_call(
        functools.partial(pack_kernel, n),
        out_shape=[jax.ShapeDtypeStruct((w // 2 + 8, w), f32)] * (n - 1),
        grid=(1,),
        in_specs=[sspec(), pl.BlockSpec((per, 1, w, w), lambda i: (0, 0, 0, 0))],
        out_specs=[vspec()] * (n - 1),
    )(neighbours, hamiltonian)
    got = [lax.ppermute(m, "narrow", pairs(k + 1, n)) for k, m in enumerate(diag_msgs)]
    dens, half, *tiles = pl.pallas_call(
        functools.partial(main_kernel, n),
        out_shape=[
            jax.ShapeDtypeStruct(hamiltonian.shape, f32),
            jax.ShapeDtypeStruct((2, w, w), f32),
        ]
        + [jax.ShapeDtypeStruct((w, w), f32)] * (n - 1),
        in_specs=[sspec()] * 3 + [vspec()] * (n + 1),
        out_specs=[vspec()] * (n + 1),
    )(neighbours, live, potential, hamiltonian, old_density, *got)
    back = [lax.ppermute(m, "narrow", pairs(k + 1, n)) for k, m in enumerate(tiles)]
    return pl.pallas_call(
        functools.partial(final_kernel, n),
        out_shape=jax.ShapeDtypeStruct(hamiltonian.shape, f32),
        in_specs=[sspec(), vspec(), pl.BlockSpec(memory_space=pl.ANY)] + [vspec()] * (n - 1),
        out_specs=pl.BlockSpec(memory_space=pl.ANY),
        scratch_shapes=[pltpu.VMEM((2, w, w), f32), pltpu.SemaphoreType.DMA((2,))],
        input_output_aliases={2: 0},
    )(neighbours, half, dens, *back)


def solution(mesh):
    placed = (
        P(("wide", "narrow"), None, None, None),
        P(("wide", "narrow"), None, None, None),
        P(("wide", "narrow"), None),
        P(("wide", "narrow")),
        P(),
    )
    return jax.shard_map(
        functools.partial(shards, mesh.shape["narrow"]),
        mesh=mesh,
        in_specs=placed,
        out_specs=P(("wide", "narrow"), None, None, None),
        check_vma=False,
    )
```

time: 74 us -> 34.5 us (0.47)
  blocking collectives: 49.2 us -> 0 us
  matrix products: 17.5 us -> 0 us
  Pallas kernels: 0 us -> 13.8 us
  starting transfers between devices: 0 us -> 10 us
  waiting for transfers between devices: 0 us -> 8.54 us
  local copies, waits for them, and re-layouts: 5.08 us -> 1.23 us
  other arithmetic: 1.06 us -> 0 us
    all_gather x3 -> x0, blocking collectives: 49.2 us -> none  [the longest x1 17.4 us: shards(): lax.all_gather(hamiltonian[:, 0], 'narrow', axis=0, tiled=True)]
    dot_general x8 -> x0, matrix products: 17.5 us -> none  [product(): return jnp.matmul(left, right, precision=lax.Precision.HIGHEST)]
    pallas_call x0 -> x3, Pallas kernels: none -> 13.8 us  [the longest x1 10.5 us: shards(): pl.pallas_call(functools.partial(main_kernel, n), out_shape=[jax.ShapeDty...]
    ppermute x0 -> x6, starting transfers between devices: none -> 10 us  [shards(): lax.ppermute(m, 'narrow', pairs(k + 1, n))]
    ppermute x0 -> x6, waiting for transfers between devices: none -> 8.54 us  [shards(): lax.ppermute(m, 'narrow', pairs(k + 1, n))]
    gather x5 -> x0, local copies, waits for them, and re-layouts: 2.32 us -> none  [the longest x2 0.65 us: shards(): from_next = jnp.take(prev_side, neighbours[:, 2], axis=0)]
    squeeze x4 -> x0, local copies, waits for them, and re-layouts: 1.33 us -> none  [the longest x1 1.1 us: assemble(): row_tiles[..., 0, :, :]]
    unnamed x8 -> x12, local copies, waits for them, and re-layouts: 0.21 us -> 1.23 us
  transfers between devices with their start and end apart: 0 -> 6, of which waited for: 0 -> 5; matrix products, arithmetic and copies ran while one was open for 0% -> 0% of each run, Pallas kernels for 0% -> 0%
where the time goes in v1:
time: 34.5 us; the launch traced here: 34.3 us
  Pallas kernels  13.8 us (40%)
  starting transfers between devices  10 us (29%)
  waiting for transfers between devices  8.54 us (25%)
  local copies, waits for them, and re-layouts  1.23 us (4%)
  between operations  0.68 us (2%)
    pallas_call x1, Pallas kernels, shards(): pl.pallas_call(functools.partial(main_kernel, n), out_shape=[jax.ShapeDty...  10.5 us
    ppermute x6, starting transfers between devices, shards(): lax.ppermute(m, 'narrow', pairs(k + 1, n))  10 us
    ppermute x6, waiting for transfers between devices, shards(): lax.ppermute(m, 'narrow', pairs(k + 1, n))  8.54 us
    pallas_call x1, Pallas kernels, shards(): pl.pallas_call(functools.partial(final_kernel, n), out_shape=jax.ShapeDty...  1.67 us
    pallas_call x1, Pallas kernels, shards(): pl.pallas_call(functools.partial(pack_kernel, n), out_shape=[jax.ShapeDty...  1.64 us
    unnamed x12, local copies, waits for them, and re-layouts  1.23 us
  transfers between devices with their start and end apart: 6, of which 5 were waited for; matrix products, arithmetic and copies ran while one was open for 0% of the time, Pallas kernels for 0%

profile of v1, /device:TPU:0, one launch (start us, length us, event | category | flops | bytes accessed | tf_op | source)
XLA Modules:
  0.0 34.3 jit_solution(7305415534629545494)
XLA Ops:
  0.0 1.6 %shard_map.55 = (f32[72,128]{1,0:T(8,128)}, f32[72,128]{1,0:T(8,128)}, f32[72,128]{1,0:T(8,128)}) custom-call(s32[2,3]{1,0:T(2,128)} %nb_ref.5, f32[2,3,128,128]{3,2,1,0:T(8,128)} %h_ref.3), custom_call_target="tpu_custom_call" | custom-call | tf_op jit(solution)/shard_map/pallas_call | solution.py:208
  1.6 3.1 %collective-permute-start = (f32[72,128]{1,0:T(8,128)}, f32[72,128]{1,0:T(8,128)S(1)}, u32[]{:S(2)}, u32[]{:S(2)}) collective-permute-start(f32[72,128]{1,0:T(8,128)} %get-tuple-element.13), channel_id=1, source_target_pairs={{0,1},{1,0},{2,3},{3,2},{4,5},{5,4},{6,7},{7,6},{8,9},{9,8},{10,11... | collective-permute-start | bytes 110600 | tf_op jit(solution)/shard_map/ppermute | solution.py:215
  4.7 2.6 %collective-permute-start.1 = (f32[72,128]{1,0:T(8,128)}, f32[72,128]{1,0:T(8,128)S(1)}, u32[]{:S(2)}, u32[]{:S(2)}) collective-permute-start(f32[72,128]{1,0:T(8,128)} %get-tuple-element.14), channel_id=1, source_target_pairs={{0,2},{1,3},{2,0},{3,1},{4,6},{5,7},{6,4},{7,5},{8,10},{9,11},{10,... | collective-permute-start | bytes 110600 | tf_op jit(solution)/shard_map/ppermute | solution.py:215
  7.3 0.0 collective-permute-start.2
  7.9 0.0 collective-permute-done.refs_0_
  8.0 0.0 copy-start.3
  8.0 2.5 %collective-permute-done.1.refs_1_ = f32[72,128]{1,0:T(8,128)S(1)} collective-permute-done((f32[72,128]{1,0:T(8,128)}, f32[72,128]{1,0:T(8,128)S(1)}, u32[]{:S(2)}, u32[]{:S(2)}) %collective-permute-start.1) | collective-permute-done | bytes 36896 | tf_op jit(solution)/shard_map/ppermute | solution.py:215
  10.4 0.0 copy-start.4
  10.4 2.8 %collective-permute-done.2.refs_2_ = f32[72,128]{1,0:T(8,128)S(1)} collective-permute-done((f32[72,128]{1,0:T(8,128)}, f32[72,128]{1,0:T(8,128)S(1)}, u32[]{:S(2)}, u32[]{:S(2)}) %collective-permute-start.2) | collective-permute-done | bytes 36896 | tf_op jit(solution)/shard_map/ppermute | solution.py:215
  13.3 0.0 copy-done.3
  13.3 0.0 copy-done.4
  13.3 0.0 copy-start.5
  13.3 0.6 %copy-done.5 = f32[72,128]{1,0:T(8,128)} copy-done((f32[72,128]{1,0:T(8,128)}, f32[72,128]{1,0:T(8,128)S(1)}, u32[]{:S(2)}) %copy-start.5) | copy-done | bytes 36888
  13.9 10.5 %shard_map.56 = (f32[2,3,128,128]{3,2,1,0:T(8,128)}, f32[2,128,128]{2,1,0:T(8,128)}, f32[128,128]{1,0:T(8,128)}, f32[128,128]{1,0:T(8,128)}, f32[128,128]{1,0:T(8,128)}) custom-call(s32[2,3]{1,0:T(2,128)} %nb_ref.5, s32[2]{0:T(128)} %live_ref.1, f32[1]{0:T(128)S(6)} %copy.8.pot_ref, f32[2,3,128,128]{3,2,1,0:T(8,128)} %h_ref.3, f32[2,3,128,128]{3,2,1,0:T(8,128)} %old_ref.1, ...), custom_call_target="tpu_custom_call" | custom-call | tf_op jit(solution)/shard_map/pallas_call | solution.py:216
  24.4 0.0 collective-permute-start.3
  24.4 1.1 %collective-permute-start.4 = (f32[128,128]{1,0:T(8,128)}, f32[128,128]{1,0:T(8,128)S(1)}, u32[]{:S(2)}, u32[]{:S(2)}) collective-permute-start(f32[128,128]{1,0:T(8,128)} %get-tuple-element.19), channel_id=1, source_target_pairs={{0,2},{1,3},{2,0},{3,1},{4,6},{5,7},{6,4},{7,5},{8,10},{9,11},{10,... | collective-permute-start | bytes 196616 | tf_op jit(solution)/shard_map/ppermute | solution.py:226
  25.4 3.3 %collective-permute-start.5 = (f32[128,128]{1,0:T(8,128)}, f32[128,128]{1,0:T(8,128)S(1)}, u32[]{:S(2)}, u32[]{:S(2)}) collective-permute-start(f32[128,128]{1,0:T(8,128)} %get-tuple-element.20), channel_id=1, source_target_pairs={{0,3},{1,2},{2,1},{3,0},{4,7},{5,6},{6,5},{7,4},{8,11},{9,10},{10,... | collective-permute-start | bytes 196616 | tf_op jit(solution)/shard_map/ppermute | solution.py:226
  28.8 0.1 collective-permute-done.3.refs_0_
  28.9 0.0 copy-start
  28.9 1.4 %collective-permute-done.4.refs_1_ = f32[128,128]{1,0:T(8,128)S(1)} collective-permute-done((f32[128,128]{1,0:T(8,128)}, f32[128,128]{1,0:T(8,128)S(1)}, u32[]{:S(2)}, u32[]{:S(2)}) %collective-permute-start.4) | collective-permute-done | bytes 65568 | tf_op jit(solution)/shard_map/ppermute | solution.py:226
  30.3 0.0 copy-start.1
  30.3 1.8 %collective-permute-done.5.refs_2_ = f32[128,128]{1,0:T(8,128)S(1)} collective-permute-done((f32[128,128]{1,0:T(8,128)}, f32[128,128]{1,0:T(8,128)S(1)}, u32[]{:S(2)}, u32[]{:S(2)}) %collective-permute-start.5) | collective-permute-done | bytes 65568 | tf_op jit(solution)/shard_map/ppermute | solution.py:226
  32.0 0.0 copy-start.2
  32.0 0.0 copy-done
  32.0 0.0 copy-done.1
  32.0 0.6 %copy-done.2 = f32[128,128]{1,0:T(8,128)} copy-done((f32[128,128]{1,0:T(8,128)}, f32[128,128]{1,0:T(8,128)S(1)}, u32[]{:S(2)}) %copy-start.2) | copy-done | bytes 65560
  32.6 1.7 %shard_map.57 = f32[2,3,128,128]{3,2,1,0:T(8,128)} custom-call(s32[2,3]{1,0:T(2,128)} %nb_ref.5, f32[2,128,128]{2,1,0:T(8,128)} %get-tuple-element.16.half_ref, f32[2,3,128,128]{3,2,1,0:T(8,128)} %get-tuple-element.17.dens_in, f32[128,128]{1,0:T(8,128)} %copy-done, f32[128,128]{1,0:T(8,128)} %copy-done.1, ...), custom_call_target="tpu_custom_call", output_to_operand_aliasing={{}: (2, {})} | custom-call | tf_op jit(solution)/shard_map/pallas_call | solution.py:227
Async XLA Ops:
  1.6 6.3 %collective-permute-start = (f32[72,128]{1,0:T(8,128)}, f32[72,128]{1,0:T(8,128)S(1)}, u32[]{:S(2)}, u32[]{:S(2)}) collective-permute-start(f32[72,128]{1,0:T(8,128)} %get-tuple-element.13), channel_id=1, source_target_pairs={{0,1},{1,0},{2,3},{3,2},{4,5},{5,4},{6,7},{7,6},{8,9},{9,8},{10,11... | collective-permute-start | bytes 110600 | tf_op jit(solution)/shard_map/ppermute | solution.py:215
  4.7 5.7 %collective-permute-start.1 = (f32[72,128]{1,0:T(8,128)}, f32[72,128]{1,0:T(8,128)S(1)}, u32[]{:S(2)}, u32[]{:S(2)}) collective-permute-start(f32[72,128]{1,0:T(8,128)} %get-tuple-element.14), channel_id=1, source_target_pairs={{0,2},{1,3},{2,0},{3,1},{4,6},{5,7},{6,4},{7,5},{8,10},{9,11},{10,... | collective-permute-start | bytes 110600 | tf_op jit(solution)/shard_map/ppermute | solution.py:215
  7.3 6.0 %collective-permute-start.2 = (f32[72,128]{1,0:T(8,128)}, f32[72,128]{1,0:T(8,128)S(1)}, u32[]{:S(2)}, u32[]{:S(2)}) collective-permute-start(f32[72,128]{1,0:T(8,128)} %get-tuple-element.15), channel_id=1, source_target_pairs={{0,3},{1,2},{2,1},{3,0},{4,7},{5,6},{6,5},{7,4},{8,11},{9,10},{10,... | collective-permute-start | bytes 110600 | tf_op jit(solution)/shard_map/ppermute | solution.py:215
  8.0 5.3 %copy-start.3 = (f32[72,128]{1,0:T(8,128)}, f32[72,128]{1,0:T(8,128)S(1)}, u32[]{:S(2)}) copy-start(f32[72,128]{1,0:T(8,128)S(1)} %collective-permute-done.refs_0_) | copy-start | bytes 110596
  10.4 2.8 %copy-start.4 = (f32[72,128]{1,0:T(8,128)}, f32[72,128]{1,0:T(8,128)S(1)}, u32[]{:S(2)}) copy-start(f32[72,128]{1,0:T(8,128)S(1)} %collective-permute-done.1.refs_1_) | copy-start | bytes 110596
  13.3 0.6 %copy-start.5 = (f32[72,128]{1,0:T(8,128)}, f32[72,128]{1,0:T(8,128)S(1)}, u32[]{:S(2)}) copy-start(f32[72,128]{1,0:T(8,128)S(1)} %collective-permute-done.2.refs_2_) | copy-start | bytes 110596
  24.4 4.5 %collective-permute-start.3 = (f32[128,128]{1,0:T(8,128)}, f32[128,128]{1,0:T(8,128)S(1)}, u32[]{:S(2)}, u32[]{:S(2)}) collective-permute-start(f32[128,128]{1,0:T(8,128)} %get-tuple-element.18), channel_id=1, source_target_pairs={{0,1},{1,0},{2,3},{3,2},{4,5},{5,4},{6,7},{7,6},{8,9},{9,8},{10,11... | collective-permute-start | bytes 196616 | tf_op jit(solution)/shard_map/ppermute | solution.py:226
  24.4 5.9 %collective-permute-start.4 = (f32[128,128]{1,0:T(8,128)}, f32[128,128]{1,0:T(8,128)S(1)}, u32[]{:S(2)}, u32[]{:S(2)}) collective-permute-start(f32[128,128]{1,0:T(8,128)} %get-tuple-element.19), channel_id=1, source_target_pairs={{0,2},{1,3},{2,0},{3,1},{4,6},{5,7},{6,4},{7,5},{8,10},{9,11},{10,... | collective-permute-start | bytes 196616 | tf_op jit(solution)/shard_map/ppermute | solution.py:226
  25.4 6.6 %collective-permute-start.5 = (f32[128,128]{1,0:T(8,128)}, f32[128,128]{1,0:T(8,128)S(1)}, u32[]{:S(2)}, u32[]{:S(2)}) collective-permute-start(f32[128,128]{1,0:T(8,128)} %get-tuple-element.20), channel_id=1, source_target_pairs={{0,3},{1,2},{2,1},{3,0},{4,7},{5,6},{6,5},{7,4},{8,11},{9,10},{10,... | collective-permute-start | bytes 196616 | tf_op jit(solution)/shard_map/ppermute | solution.py:226
  28.9 3.2 %copy-start = (f32[128,128]{1,0:T(8,128)}, f32[128,128]{1,0:T(8,128)S(1)}, u32[]{:S(2)}) copy-start(f32[128,128]{1,0:T(8,128)S(1)} %collective-permute-done.3.refs_0_) | copy-start | bytes 196612
  30.3 1.8 %copy-start.1 = (f32[128,128]{1,0:T(8,128)}, f32[128,128]{1,0:T(8,128)S(1)}, u32[]{:S(2)}) copy-start(f32[128,128]{1,0:T(8,128)S(1)} %collective-permute-done.4.refs_1_) | copy-start | bytes 196612
  32.0 0.6 %copy-start.2 = (f32[128,128]{1,0:T(8,128)}, f32[128,128]{1,0:T(8,128)S(1)}, u32[]{:S(2)}) copy-start(f32[128,128]{1,0:T(8,128)S(1)} %collective-permute-done.5.refs_2_) | copy-start | bytes 196612
